TPU v7x, 32 devices: a whole 2x2x4 slice. The times are simulated.
32 devices in a mesh: dp: 16 (over z, y, core), tensor: 2 (over x).
Axes of the slice: x: 2, y: 2, z: 4, core: 2. Of those that a mesh axis runs over, the one named last changes fastest.
Arguments:
- tokens: float32 [2, 25600, 512], P(None, ('dp', 'tensor')), may hold values from -6 to 6
- key_mask: int32 [2, 128, 200], P(None, 'dp'), may hold values from 0 to 1, as said below
- expert_ids: int32 [2, 25600, 2], P(None, 'dp'), may hold values from 0 to 31, as said below
- slot_ids: int32 [2, 25600, 2], P(None, 'dp'), may hold values from -1 to 119, as said below
- norm1_gain: float32 [512], P(('dp', 'tensor')), may hold values from 0.25 to 1.75
- norm1_bias: float32 [512], P(('dp', 'tensor')), may hold values from -3 to 3
- qkv_weight: bfloat16 [512, 3, 512], P('dp', None, 'tensor'), may hold values from -0.25 to 0.25
- out_weight: bfloat16 [512, 512], P('tensor', 'dp'), may hold values from -1 to 1
- norm2_gain: float32 [512], P(('dp', 'tensor')), may hold values from 0.25 to 1.75
- norm2_bias: float32 [512], P(('dp', 'tensor')), may hold values from -3 to 3
- router_weight: float32 [512, 32], P(('dp', 'tensor')), may hold values from -0.25 to 0.25
- expert_in: bfloat16 [32, 512, 2048], P(None, 'dp', 'tensor'), may hold values from -0.25 to 0.25
- expert_out: bfloat16 [32, 2048, 512], P(None, 'tensor', 'dp'), may hold values from -3 to 3
- cotangent: float32 [2, 25600, 512], P(None, ('dp', 'tensor')), may hold values from -6 to 6
Outputs:
- block_out: float32 [2, 25600, 512], P(None, ('dp', 'tensor'))
- input_grad: float32 [2, 25600, 512], P(None, ('dp', 'tensor'))
- norm1_gain_grad: float32 [512], P(('dp', 'tensor'))
- norm1_bias_grad: float32 [512], P(('dp', 'tensor'))
- qkv_grad: float32 [512, 3, 512], P('dp', None, 'tensor')
- out_grad: float32 [512, 512], P('tensor', 'dp')
- norm2_gain_grad: float32 [512], P(('dp', 'tensor'))
- norm2_bias_grad: float32 [512], P(('dp', 'tensor'))
- router_grad: float32 [512, 32], P(('dp', 'tensor'))
- expert_in_grad: float32 [32, 512, 2048], P(None, 'dp', 'tensor')
- expert_out_grad: float32 [32, 2048, 512], P(None, 'tensor', 'dp')
Inputs may be any that keep to these rules, and one draw needn't show every extreme that they name: `key_mask`: position 0 of every image is 1; positions 197 to 199 are 0. `expert_ids`: each row names two different experts. `slot_ids`: slots count within routing groups of 1600 consecutive rows of a micro-batch. -1 marks a dropped route; no two other routes of a group share expert and slot, and the slots used by one expert in a group are 0, 1, 2, ... without gaps.
All inputs are finite; a program needn't handle non-finite values.
Results may differ from a plain program's by a relative error of at most 0.035.
Values may be sent and summed in bfloat16 or wider, within the bound.
A program may use at most 264 MiB of HBM per device.

v0:
```python
import functools

import jax
import jax.numpy as jnp
from jax import lax
from jax.experimental import pallas as pl
from jax.experimental.pallas import tpu as pltpu
from jax.sharding import Mesh, PartitionSpec as P

HEAD = 64
CAP = 120
EPSILON = 1e-06
LANES = 128
VMEM = 60 * 1024 * 1024
NN = (((1,), (0,)), ((), ()))
NT = (((1,), (1,)), ((), ()))
TN = (((0,), (0,)), ((), ()))
HIGH = lax.Precision.HIGHEST
GELU_C = 0.7978845608028654
GELU_A = 0.044715


def mm(a, b, dims=NN, precision=None):
    return lax.dot_general(a, b, dims, precision=precision, preferred_element_type=jnp.float32)


def three_parts(value):
    high = value.astype(jnp.bfloat16)
    rest = value - high.astype(jnp.float32)
    middle = rest.astype(jnp.bfloat16)
    last = (rest - middle.astype(jnp.float32)).astype(jnp.bfloat16)
    return high, middle, last


def standardize(values):
    center = jnp.mean(values, -1, keepdims=True)
    shifted = values - center
    spread = jnp.mean(shifted * shifted, -1, keepdims=True)
    inverse = lax.rsqrt(spread + EPSILON)
    return shifted * inverse, inverse


def norm_back(grad, unit, inverse):
    return inverse * (
        grad
        - jnp.mean(grad, -1, keepdims=True)
        - unit * jnp.mean(grad * unit, -1, keepdims=True)
    )


def even_lanes(shape):
    return lax.broadcasted_iota(jnp.int32, shape, 1) < HEAD


def router_gates(routed, parts):
    logits = mm(routed, parts, NT)
    logits = logits + pltpu.roll(logits, LANES - 32, 1) + pltpu.roll(logits, LANES - 64, 1)
    lane = lax.broadcasted_iota(jnp.int32, logits.shape, 1)
    logits = jnp.where(lane < 32, logits, -1e30)
    lifted = jnp.exp(logits - jnp.max(logits, -1, keepdims=True))
    return lifted / jnp.sum(lifted, -1, keepdims=True)


def forward_rows(first, images, tok_ref, bias_ref, mats_ref, norms_ref, parts_ref,
                 middle_ref, proj_ref, mixed_ref, gates_ref):
    _, length, width = tok_ref.shape
    pieces, _, _, columns = mats_ref.shape
    rows = images * length
    here = pl.ds(first, images)
    tok = tok_ref[here].reshape(rows, width)
    unit, _ = standardize(tok)
    normed = (unit * norms_ref[0:1] + norms_ref[1:2]).astype(jnp.bfloat16)
    for c in range(3):
        for p in range(pieces):
            part = mm(normed, mats_ref[p, c]).reshape(images, length, columns)
            base = c * width + p * columns
            for b in range(images):
                proj_ref[first + b, :, base:base + columns] = part[b].astype(jnp.bfloat16)
    even = even_lanes((length, LANES))
    scale = jnp.bfloat16(HEAD ** -0.5)
    zero = jnp.zeros((), jnp.bfloat16)
    attended = []
    for b in range(images):
        bias = bias_ref[first + b]
        parts = []
        for pair in range(width // LANES):
            lanes = slice(pair * LANES, (pair + 1) * LANES)
            query = proj_ref[first + b, :, lanes] * scale
            keyed = proj_ref[first + b, :, width + pair * LANES:width + (pair + 1) * LANES]
            valued = proj_ref[first + b, :, 2 * width + pair * LANES:2 * width + (pair + 1) * LANES]
            halves = []
            for odd in range(2):
                chosen = jnp.where(even != bool(odd), query, zero)
                scores = mm(chosen, keyed, NT) + bias
                lifted = jnp.exp(scores - jnp.max(scores, -1, keepdims=True))
                probs = lifted * (1.0 / jnp.sum(lifted, -1, keepdims=True))
                halves.append(mm(probs.astype(jnp.bfloat16), valued))
            both = jnp.where(even, halves[0], halves[1])
            mixed_ref[first + b, :, lanes] = both.astype(jnp.bfloat16)
            parts.append(both)
        attended.append(jnp.concatenate(parts, 1))
    joined = jnp.concatenate(attended, 0).astype(jnp.bfloat16)
    middle = tok
    for p in range(pieces):
        middle += mm(joined[:, p * columns:(p + 1) * columns], mats_ref[p, 3], NT)
    middle_ref[here] = middle.reshape(images, length, width)
    unit, _ = standardize(middle)
    routed = unit * norms_ref[2:3] + norms_ref[3:4]
    low = routed.astype(jnp.bfloat16)
    gates_ref[here] = router_gates(low, parts_ref[...]).reshape(images, length, LANES)
    return routed, low


def forward_kernel(
    tok_ref, bias_ref, mats_ref, norms_ref, parts_ref,
    middle_ref, routed_ref, proj_ref, mixed_ref, gates_ref,
):
    images, length, width = tok_ref.shape
    routed, _ = forward_rows(0, images, tok_ref, bias_ref, mats_ref, norms_ref, parts_ref,
                             middle_ref, proj_ref, mixed_ref, gates_ref)
    routed_ref[...] = routed.reshape(images, length, width).astype(jnp.bfloat16)


def attention_forward(tok, bias, mats, norms, router, per_step):
    images, length, width = tok.shape

    def rows(last):
        return pl.BlockSpec((per_step, length, last), lambda s: (s, 0, 0))

    def whole(a):
        return pl.BlockSpec(a.shape, lambda s: (0,) * a.ndim)

    shapes = [
        (width, jnp.float32), (width, jnp.bfloat16), (3 * width, jnp.bfloat16),
        (width, jnp.bfloat16), (LANES, jnp.float32),
    ]
    return pl.pallas_call(
        forward_kernel,
        grid=(images // per_step,),
        in_specs=[
            rows(width), pl.BlockSpec((per_step, 1, length), lambda s: (s, 0, 0)),
            whole(mats), whole(norms), whole(router),
        ],
        out_specs=[rows(n) for n, _ in shapes],
        out_shape=[jax.ShapeDtypeStruct((images, length, n), kind) for n, kind in shapes],
        compiler_params=pltpu.CompilerParams(vmem_limit_bytes=VMEM),
        cost_estimate=pl.CostEstimate(
            flops=images * length * width * width * 10, bytes_accessed=images * length * width * 16,
            transcendentals=images * length * length * 8),
        name="attention_forward",
    )(tok, bias, mats, norms, router)


def backward_rows(first, images, grad, tok_ref, middle_ref, cot_ref, gates_ref, proj_ref, mixed_ref,
                  bias_ref, mats_ref, norms_ref, router_t_ref,
                  input_ref, dnorms_ref, drouter_ref, dproj_ref, dmats_acc):
    _, length, width = tok_ref.shape
    rows = images * length
    here = pl.ds(first, images)

    def flat(ref):
        return ref[here].reshape(rows, ref.shape[2])

    middle = flat(middle_ref)
    unit, inverse = standardize(middle)
    gates = flat(gates_ref)
    gate_cot = grad[:, width:]
    logit_grad = gates * (gate_cot - jnp.sum(gates * gate_cot, -1, keepdims=True))
    routed = (unit * norms_ref[2:3] + norms_ref[3:4]).astype(jnp.bfloat16)
    drouter_ref[...] += mm(routed.astype(jnp.float32), logit_grad, TN, HIGH)
    routed_grad = grad[:, :width] + mm(logit_grad, router_t_ref[...], NN, HIGH)
    dnorms_ref[2:3] += jnp.sum(routed_grad * unit, 0, keepdims=True)
    dnorms_ref[3:4] += jnp.sum(routed_grad, 0, keepdims=True)
    middle_grad = flat(cot_ref) + norm_back(routed_grad * norms_ref[2:3], unit, inverse)
    attn_cot = middle_grad.astype(jnp.bfloat16)
    joined = jnp.concatenate([mixed_ref[first + b].astype(jnp.float32) for b in range(images)], 0)
    joined = joined.astype(jnp.bfloat16)
    pieces, _, _, columns = mats_ref.shape
    spans = [slice(p * columns, (p + 1) * columns) for p in range(pieces)]
    for p in range(pieces):
        dmats_acc[p, 3] += mm(attn_cot, joined[:, spans[p]], TN)
    mixed_grad = jnp.concatenate([mm(attn_cot, mats_ref[p, 3]) for p in range(pieces)], 1)
    mixed_grad = mixed_grad.reshape(images, length, width)
    even = even_lanes((length, LANES))
    zero = jnp.zeros((), jnp.bfloat16)
    scale = jnp.bfloat16(HEAD ** -0.5)
    for b in range(images):
        bias = bias_ref[first + b]
        mixed_low = mixed_grad[b].astype(jnp.bfloat16)
        for pair in range(width // LANES):
            lanes = slice(pair * LANES, (pair + 1) * LANES)
            query = proj_ref[first + b, :, lanes] * scale
            keyed = proj_ref[first + b, :, width + pair * LANES:width + (pair + 1) * LANES]
            valued = proj_ref[first + b, :, 2 * width + pair * LANES:2 * width + (pair + 1) * LANES]
            out_cot = mixed_low[:, lanes]
            query_grad = keyed_grad = value_grad = None
            for odd in range(2):
                mask = even != bool(odd)
                query_half = jnp.where(mask, query, zero)
                keyed_half = jnp.where(mask, keyed, zero)
                cot_half = jnp.where(mask, out_cot, zero)
                scores = mm(query_half, keyed, NT) + bias
                lifted = jnp.exp(scores - jnp.max(scores, -1, keepdims=True))
                probs = lifted * (1.0 / jnp.sum(lifted, -1, keepdims=True))
                prob_grad = mm(cot_half, valued, NT)
                value_part = mm(probs.astype(jnp.bfloat16), cot_half, TN)
                inner = jnp.sum(probs * prob_grad, -1, keepdims=True)
                score_grad = (probs * (prob_grad - inner)).astype(jnp.bfloat16)
                query_part = mm(score_grad, keyed_half)
                keyed_part = mm(score_grad, query_half, TN)
                if odd:
                    query_grad, keyed_grad, value_grad = (
                        query_grad + query_part, keyed_grad + keyed_part, value_grad + value_part)
                else:
                    query_grad, keyed_grad, value_grad = query_part, keyed_part, value_part
            base = pair * LANES
            rows_here = slice(b * length, (b + 1) * length)
            dproj_ref[rows_here, base:base + LANES] = query_grad * (HEAD ** -0.5)
            dproj_ref[rows_here, width + base:width + base + LANES] = keyed_grad
            dproj_ref[rows_here, 2 * width + base:2 * width + base + LANES] = value_grad
    tok = flat(tok_ref)
    unit, inverse = standardize(tok)
    normed = (unit * norms_ref[0:1] + norms_ref[1:2]).astype(jnp.bfloat16)
    normed_grad = jnp.zeros((rows, width), jnp.float32)
    for c in range(3):
        part = dproj_ref[:, c * width:(c + 1) * width].astype(jnp.bfloat16)
        for p in range(pieces):
            dmats_acc[p, c] += mm(normed, part[:, spans[p]], TN)
            normed_grad += mm(part[:, spans[p]], mats_ref[p, c], NT)
    dnorms_ref[0:1] += jnp.sum(normed_grad * unit, 0, keepdims=True)
    dnorms_ref[1:2] += jnp.sum(normed_grad, 0, keepdims=True)
    input_grad = middle_grad + norm_back(normed_grad * norms_ref[0:1], unit, inverse)
    input_ref[here] = input_grad.reshape(images, length, width)


def backward_kernel(
    tok_ref, middle_ref, cot_ref, grad_ref, gates_ref, proj_ref, mixed_ref,
    bias_ref, mats_ref, norms_ref, router_t_ref,
    input_ref, dmats_ref, dnorms_ref, drouter_ref,
    dproj_ref, dmats_acc,
):
    images, length, width = tok_ref.shape
    rows = images * length
    step = pl.program_id(0)

    @pl.when(step == 0)
    def _():
        dmats_acc[...] = jnp.zeros_like(dmats_acc)
        dnorms_ref[...] = jnp.zeros_like(dnorms_ref)
        drouter_ref[...] = jnp.zeros_like(drouter_ref)

    backward_rows(0, images, grad_ref[...].reshape(rows, grad_ref.shape[2]), tok_ref, middle_ref, cot_ref,
                  gates_ref, proj_ref, mixed_ref, bias_ref, mats_ref, norms_ref, router_t_ref,
                  input_ref, dnorms_ref, drouter_ref, dproj_ref, dmats_acc)

    @pl.when(step == pl.num_programs(0) - 1)
    def _():
        dmats_ref[...] = dmats_acc[...].astype(jnp.bfloat16)


def attention_backward(tok, middle, cot, grad, gates, proj, mixed, bias, mats, norms, router_t, per_step):
    images, length, width = tok.shape

    def rows(last):
        return pl.BlockSpec((per_step, length, last), lambda s: (s, 0, 0))

    def whole(shape):
        return pl.BlockSpec(shape, lambda s: (0,) * len(shape))

    return pl.pallas_call(
        backward_kernel,
        grid=(images // per_step,),
        in_specs=[
            rows(width), rows(width), rows(width), rows(width + LANES), rows(LANES),
            rows(3 * width), rows(width), pl.BlockSpec((per_step, 1, length), lambda s: (s, 0, 0)),
            whole(mats.shape), whole(norms.shape), whole(router_t.shape),
        ],
        out_specs=[
            rows(width), whole(mats.shape), whole((4, width)), whole((width, LANES)),
        ],
        out_shape=[
            jax.ShapeDtypeStruct((images, length, width), jnp.float32),
            jax.ShapeDtypeStruct(mats.shape, jnp.bfloat16),
            jax.ShapeDtypeStruct((4, width), jnp.float32),
            jax.ShapeDtypeStruct((width, LANES), jnp.float32),
        ],
        scratch_shapes=[
            pltpu.VMEM((per_step * length, 3 * width), jnp.float32),
            pltpu.VMEM(mats.shape, jnp.float32),
        ],
        compiler_params=pltpu.CompilerParams(vmem_limit_bytes=VMEM),
        cost_estimate=pl.CostEstimate(
            flops=images * length * width * width * 30, bytes_accessed=images * length * width * 30,
            transcendentals=images * length * length * 8),
        name="attention_backward",
    )(tok, middle, cot, grad, gates, proj, mixed, bias, mats, norms, router_t)


def expert_kernel(
    expert_ref, slots_ref, cots_ref, weights_ref, router_ref,
    result_ref, back_ref, dweights_ref,
    rows_t, grads_t, grads, gate_scr, result_acc, back_acc, first_acc, second_acc,
):
    count, width = slots_ref.shape
    tile = weights_ref.shape[-1]
    chunk = rows_t.shape[2]
    step = pl.program_id(0)
    first = weights_ref[:, :, 0, 0].reshape(width, tile)
    second = weights_ref[:, :, 0, 1].reshape(width, tile)

    @pl.when(step == 0)
    def _():
        def prepare(r, carry):
            here = pl.ds(pl.multiple_of(r * chunk, 16), chunk)
            slots = slots_ref[here]
            gates = router_gates(slots, router_ref[...])
            lane = lax.broadcasted_iota(jnp.int32, gates.shape, 1)
            gate = jnp.sum(jnp.where(lane == expert_ref[0], gates, 0.0), -1, keepdims=True)
            gate_scr[here] = jnp.broadcast_to(gate, gates.shape)
            low = (cots_ref[here].astype(jnp.float32) * gate).astype(jnp.bfloat16)
            grads[here] = low
            rows_t[r] = slots.T
            grads_t[r] = low.T
            result_acc[here] = jnp.zeros((chunk, width), jnp.float32)
            back_acc[here] = jnp.zeros((chunk, width), jnp.float32)
            return carry

        lax.fori_loop(0, count // chunk, prepare, 0)

    first_acc[...] = jnp.zeros_like(first_acc)
    second_acc[...] = jnp.zeros_like(second_acc)

    def work(r, carry):
        here = pl.ds(pl.multiple_of(r * chunk, 16), chunk)
        pre = mm(slots_ref[here], first)
        square = pre * pre
        half = 0.5 + 0.5 * jnp.tanh(pre * (GELU_C + (GELU_C * GELU_A) * square))
        hidden = (pre * half).astype(jnp.bfloat16)
        slope = half + 2.0 * half * (1.0 - half) * pre * (GELU_C + (3.0 * GELU_C * GELU_A) * square)
        hidden_grad = mm(grads[here], second)
        pre_grad = (hidden_grad * slope).astype(jnp.bfloat16)
        result_acc[here] += mm(hidden, second, NT)
        back_acc[here] += mm(pre_grad, first, NT)
        first_acc[...] += mm(rows_t[r], pre_grad)
        second_acc[...] += mm(grads_t[r], hidden)
        return carry

    lax.fori_loop(0, count // chunk, work, 0)
    block = weights_ref.shape[:2] + weights_ref.shape[4:]
    dweights_ref[:, :, 0, 0] = first_acc[...].astype(jnp.bfloat16).reshape(block)
    dweights_ref[:, :, 0, 1] = second_acc[...].astype(jnp.bfloat16).reshape(block)

    @pl.when(step == pl.num_programs(0) - 1)
    def _():
        def finish(r, carry):
            here = pl.ds(pl.multiple_of(r * chunk, 16), chunk)
            result = result_acc[here]
            gate = gate_scr[here][:, 0:1]
            result_ref[here] = (result * gate).astype(jnp.bfloat16)
            gate_grad = jnp.sum(cots_ref[here].astype(jnp.float32) * result, -1, keepdims=True)
            lane = lax.broadcasted_iota(jnp.int32, (chunk, LANES), 1)
            back_ref[here, 0:width] = back_acc[here].astype(jnp.bfloat16)
            back_ref[here, width:width + LANES] = jnp.where(
                lane == expert_ref[0], gate_grad, 0.0).astype(jnp.bfloat16)
            return carry

        lax.fori_loop(0, count // chunk, finish, 0)


def run_expert(expert, slots, cots, weights, router):
    count, width = slots.shape
    planes, inner, parts, _, depth, extent = weights.shape
    tile = min(512, extent)
    per_part = extent // tile
    chunk = 480

    def whole(shape):
        return pl.BlockSpec(shape, lambda s, e: (0,) * len(shape))

    weight_spec = pl.BlockSpec(
        (planes, inner, 1, 2, depth, tile), lambda s, e: (0, 0, s // per_part, 0, 0, s % per_part))
    return pl.pallas_call(
        expert_kernel,
        grid_spec=pltpu.PrefetchScalarGridSpec(
            num_scalar_prefetch=1,
            grid=(parts * per_part,),
            in_specs=[whole(slots.shape), whole(cots.shape), weight_spec, whole(router.shape)],
            out_specs=[whole((count, width)), whole((count, width + LANES)), weight_spec],
            scratch_shapes=[
                pltpu.VMEM((count // chunk, width, chunk), jnp.bfloat16),
                pltpu.VMEM((count // chunk, width, chunk), jnp.bfloat16),
                pltpu.VMEM((count, width), jnp.bfloat16),
                pltpu.VMEM((count, LANES), jnp.float32),
                pltpu.VMEM((count, width), jnp.float32),
                pltpu.VMEM((count, width), jnp.float32),
                pltpu.VMEM((width, tile), jnp.float32),
                pltpu.VMEM((width, tile), jnp.float32),
            ],
        ),
        out_shape=[
            jax.ShapeDtypeStruct((count, width), jnp.bfloat16),
            jax.ShapeDtypeStruct((count, width + LANES), jnp.bfloat16),
            jax.ShapeDtypeStruct(weights.shape, jnp.bfloat16),
        ],
        compiler_params=pltpu.CompilerParams(vmem_limit_bytes=VMEM),
        cost_estimate=pl.CostEstimate(
            flops=12 * count * width * extent * parts,
            bytes_accessed=4 * 2 * width * extent * parts + count * width * 8,
            transcendentals=count * extent * parts),
        name="expert",
    )(expert, slots, cots, weights, router)


def flipped(position, bit):
    return position + bit - 2 * bit * lax.rem(position // bit, 2)


def to_peer(source, target, sends, receives, where):
    return pltpu.make_async_remote_copy(
        src_ref=source, dst_ref=target, send_sem=sends, recv_sem=receives, device_id=where,
        device_id_type=pl.DeviceIdType.MESH)


class Dispatch:
    def __init__(self, index_ref, shared, staged, out, sends, receives, keep, inner, parts, local):
        self.index_ref, self.shared, self.staged, self.out = index_ref, shared, staged, out
        self.sends, self.receives, self.keep = sends, receives, keep
        self.inner, self.parts, self.local = inner, parts, local
        self.at_i, self.at_t = lax.axis_index("i"), lax.axis_index("t")

    def copy(self, m, d, k):
        home = lax.rem(self.at_i + d, self.inner)
        target = self.out.at[k, pl.ds(pl.multiple_of((m * self.inner + self.at_i) * CAP, 8), CAP)]
        return to_peer(self.staged.at[m, d, k], target, self.sends.at[m, d, k],
                       self.receives.at[m, d, k], {"i": home})

    def kept(self, m, k):
        target = self.out.at[k, pl.ds(pl.multiple_of((m * self.inner + self.at_i) * CAP, 8), CAP)]
        return pltpu.make_async_copy(self.staged.at[m, 0, k], target, self.keep.at[m, k])

    def fill(self, m, d):
        home = lax.rem(self.at_i + d, self.inner)
        count = self.local * CAP
        base = (home * self.parts + self.at_t) * count
        places = base + lax.broadcasted_iota(jnp.int32, (count, 1), 0)
        total = None
        for half in range(2):
            first = self.index_ref[m, 0, half:half + 1]
            second = self.index_ref[m, 1, half:half + 1]
            hits = jnp.where((first == places) | (second == places), 1.0, 0.0).astype(jnp.bfloat16)
            part = mm(hits, self.shared[m, half])
            total = part if total is None else total + part
        for k in range(self.local):
            self.staged[m, d, k] = total[k * CAP:(k + 1) * CAP].astype(jnp.bfloat16)

    def send(self, m):
        def step(d, carry):
            self.fill(m, d)
            for k in range(self.local):
                self.copy(m, d, k).start()
            return carry

        lax.fori_loop(1, self.inner, step, 0)
        self.fill(m, 0)
        for k in range(self.local):
            self.kept(m, k).start()

    def finish(self, m):
        def step(d, carry):
            for k in range(self.local):
                self.copy(m, d, k).wait()
            return carry

        lax.fori_loop(1, self.inner, step, 0)
        for k in range(self.local):
            self.kept(m, k).wait()


def flipped_if(position, bit, on):
    return position + on * (bit - 2 * bit * lax.rem(position // bit, 2))


class Answer:
    def __init__(self, staged, out, sends, receives, keep, inner):
        self.staged, self.out, self.sends, self.receives, self.keep = staged, out, sends, receives, keep
        self.inner = inner
        self.at_i = lax.axis_index("i")

    def target(self, k, m):
        return self.out.at[k, m, pl.ds(pl.multiple_of(self.at_i * CAP, 8), CAP)]

    def copy(self, k, m, d):
        group = lax.rem(self.at_i + d, self.inner)
        return to_peer(self.staged.at[m, group, k], self.target(k, m), self.sends.at[k, m, d],
                       self.receives.at[k, m, d], {"i": group})

    def kept(self, k, m):
        return pltpu.make_async_copy(self.staged.at[m, self.at_i, k], self.target(k, m), self.keep.at[k, m])

    def send(self, k, m):
        def step(d, carry):
            self.copy(k, m, d).start()
            return carry

        lax.fori_loop(1, self.inner, step, 0)
        self.kept(k, m).start()

    def finish(self, k, m):
        def step(d, carry):
            self.copy(k, m, d).wait()
            return carry

        lax.fori_loop(1, self.inner, step, 0)
        self.kept(k, m).wait()


def device_at(n, origin):
    o, i, t = origin
    return lax.rem(o + n // 16, 2), lax.rem(i + lax.rem(n // 2, 8), 8), lax.rem(t + lax.rem(n, 2), 2)


class Weights:
    def __init__(self, local, sources, target, sends, receives, keep):
        self.local, self.sources, self.target = local, sources, target
        self.sends, self.receives, self.keep = sends, receives, keep
        self.origin = tuple(lax.axis_index(name) for name in ("o", "i", "t"))

    def place(self, k, part):
        o, i, t = self.origin
        return self.target.at[k, o, i, t, part]

    def copy(self, k, n, part):
        o, i, t = device_at(n, self.origin)
        expert = (i * 2 + t) * self.local + k
        return to_peer(self.sources[part].at[expert], self.place(k, part), self.sends.at[k, n, part],
                       self.receives.at[k, n, part], {"o": o, "i": i, "t": t})

    def kept(self, k, part):
        _, i, t = self.origin
        expert = (i * 2 + t) * self.local + k
        return pltpu.make_async_copy(
            self.sources[part].at[expert], self.place(k, part), self.keep.at[k, part])

    def send(self, k):
        def step(n, carry):
            for part in range(2):
                self.copy(k, 32 - n, part).start()
            return carry

        lax.fori_loop(1, 32, step, 0)
        for part in range(2):
            self.kept(k, part).start()

    def finish(self, k):
        def step(n, carry):
            for part in range(2):
                self.copy(k, n, part).wait()
            return carry

        lax.fori_loop(1, 32, step, 0)
        for part in range(2):
            self.kept(k, part).wait()


class Gradients:
    def __init__(self, local, source, target, sends, receives, keep):
        self.local, self.source, self.target = local, source, target
        self.sends, self.receives, self.keep = sends, receives, keep
        self.origin = tuple(lax.axis_index(name) for name in ("o", "i", "t"))

    def place(self, k, part):
        o, i, t = self.origin
        return self.target.at[o, (i * 2 + t) * self.local + k, part]

    def copy(self, k, n, part):
        o, i, t = device_at(n, self.origin)
        return to_peer(self.source.at[k, o, i, t, part], self.place(k, part), self.sends.at[k, n, part],
                       self.receives.at[k, n, part], {"o": o, "i": i, "t": t})

    def kept(self, k, part):
        o, i, t = self.origin
        return pltpu.make_async_copy(
            self.source.at[k, o, i, t, part], self.place(k, part), self.keep.at[k, part])

    send = Weights.send
    finish = Weights.finish


def expert_scratch(count, width, tile, chunk):
    steps = count // chunk
    return [
        pltpu.VMEM((count, width), jnp.bfloat16), pltpu.VMEM((count, width), jnp.bfloat16),
        pltpu.VMEM((steps, width, chunk), jnp.bfloat16), pltpu.VMEM((steps, width, chunk), jnp.bfloat16),
        pltpu.VMEM((count, width), jnp.bfloat16), pltpu.VMEM((count, LANES), jnp.float32),
        pltpu.VMEM((count, width), jnp.float32), pltpu.VMEM((count, width), jnp.float32),
        pltpu.VMEM((2, width, tile), jnp.float32), pltpu.VMEM((2, width, tile), jnp.bfloat16),
        pltpu.SemaphoreType.DMA((2,)),
    ]


def expert_phase(k, expert, slots_hbm, cots_hbm, held, parts_ref, answers, scratch):
    slots, cots, rows_t, grads_t, grads, gate_scr, result_acc, back_acc, sums, tiles, load = scratch
    count, width = slots.shape
    chunk = rows_t.shape[2]
    tile = tiles.shape[2]
    micros, groups = answers[0].staged.shape[:2]
    loads = [pltpu.make_async_copy(slots_hbm.at[k], slots, load.at[0]),
             pltpu.make_async_copy(cots_hbm.at[k], cots, load.at[1])]
    for copy in loads:
        copy.start()
    for copy in loads:
        copy.wait()

    def prepare(r, carry):
        here = pl.ds(pl.multiple_of(r * chunk, 16), chunk)
        rows = slots[here]
        gates = router_gates(rows, parts_ref[...])
        lane = lax.broadcasted_iota(jnp.int32, gates.shape, 1)
        gate = jnp.sum(jnp.where(lane == expert, gates, 0.0), -1, keepdims=True)
        gate_scr[here] = jnp.broadcast_to(gate, gates.shape)
        low = (cots[here].astype(jnp.float32) * gate).astype(jnp.bfloat16)
        grads[here] = low
        rows_t[r] = rows.T
        grads_t[r] = low.T
        result_acc[here] = jnp.zeros((chunk, width), jnp.float32)
        back_acc[here] = jnp.zeros((chunk, width), jnp.float32)
        return carry

    lax.fori_loop(0, count // chunk, prepare, 0)
    per_part = held.shape[6] // tile

    def one_tile(n, carry):
        t = n // per_part
        span = pl.ds(pl.multiple_of(lax.rem(n, per_part) * tile, tile), tile)
        for part in range(2):
            tiles[part] = held[k, :, :, t, part, :, span].reshape(width, tile)
        sums[...] = jnp.zeros_like(sums)

        def work(r, inside):
            here = pl.ds(pl.multiple_of(r * chunk, 16), chunk)
            pre = mm(slots[here], tiles[0])
            square = pre * pre
            half = 0.5 + 0.5 * jnp.tanh(pre * (GELU_C + (GELU_C * GELU_A) * square))
            hidden = (pre * half).astype(jnp.bfloat16)
            slope = half + 2.0 * half * (1.0 - half) * pre * (
                GELU_C + (3.0 * GELU_C * GELU_A) * square)
            pre_grad = (mm(grads[here], tiles[1]) * slope).astype(jnp.bfloat16)
            result_acc[here] += mm(hidden, tiles[1], NT)
            back_acc[here] += mm(pre_grad, tiles[0], NT)
            sums[0] += mm(rows_t[r], pre_grad)
            sums[1] += mm(grads_t[r], hidden)
            return inside

        lax.fori_loop(0, count // chunk, work, 0)
        block = held.shape[1:3] + (held.shape[5], tile)
        for part in range(2):
            held[k, :, :, t, part, :, span] = sums[part].astype(jnp.bfloat16).reshape(block)
        return carry

    lax.fori_loop(0, held.shape[3] * per_part, one_tile, 0)
    per_chunk = chunk // CAP
    back, result = answers

    def finish(n, carry):
        here = pl.ds(pl.multiple_of(n * chunk, 16), chunk)
        m, r = n // (groups // per_chunk), lax.rem(n, groups // per_chunk)
        value = result_acc[here]
        gate_grad = jnp.sum(cots[here].astype(jnp.float32) * value, -1, keepdims=True)
        lane = lax.broadcasted_iota(jnp.int32, (chunk, LANES), 1)
        spread = jnp.where(lane == expert, gate_grad, 0.0)
        value = value * gate_scr[here][:, 0:1]
        grad = back_acc[here]
        for q in range(per_chunk):
            rows = slice(q * CAP, (q + 1) * CAP)
            at = r * per_chunk + q
            result.staged[m, at, k] = value[rows].astype(jnp.bfloat16)
            back.staged[m, at, k, :, 0:width] = grad[rows].astype(jnp.bfloat16)
            back.staged[m, at, k, :, width:width + LANES] = spread[rows].astype(jnp.bfloat16)
        return carry

    lax.fori_loop(0, micros * groups // per_chunk, finish, 0)
    for m in range(micros):
        back.send(k, m)
    for m in range(micros):
        result.send(k, m)


def opening_kernel(
    local, per_step, pack_ref, cot_ref, index_ref, table_ref, tok_ref, bias_ref, first_ref, second_ref,
    small_ref, block_out, input_out, dweights_ref, middle_out, proj_out, mixed_out, gates_out,
    slots_ref, cots_ref, back_ref, result_ref,
    gathered, partial, loose, mats_ref, norms_ref, parts_ref, router_ref, shared_c, shared_r, away_g,
    staged_c, staged_r, held, staged_back,
    load, ring_send, ring_recv, pair_send, pair_recv, pair_send_r, pair_recv_r,
    cot_send, cot_recv, cot_keep, row_send, row_recv, row_keep,
    weight_send, weight_recv, weight_keep, grad_send, grad_recv, grad_keep,
    back_send, back_recv, back_keep, result_send, result_recv, result_keep, store,
    away_send, away_recv, fold_send, fold_recv, fetch,
):
    at_o, at_i, at_t = (lax.axis_index(name) for name in ("o", "i", "t"))
    micros, _, own_rows, width = shared_c.shape
    images, length, _ = tok_ref.shape
    kinds, columns = mats_ref.shape[1], mats_ref.shape[3]
    depth = width // 16
    rows = per_step * length
    steps = own_rows // rows
    stages = [
        {"t": 1 - at_t}, {"o": 1 - at_o}, {"i": flipped(at_i, 4)}, {"i": flipped(at_i, 2)},
        {"i": flipped(at_i, 1)},
    ]
    cot_plan = Dispatch(index_ref, shared_c, staged_c, cots_ref, cot_send, cot_recv, cot_keep, 8, 2, local)
    row_plan = Dispatch(index_ref, shared_r, staged_r, slots_ref, row_send, row_recv, row_keep, 8, 2, local)
    weights = Weights(local, (first_ref, second_ref), held, weight_send, weight_recv, weight_keep)
    gradients = Gradients(local, held, dweights_ref, grad_send, grad_recv, grad_keep)

    def stage(j):
        size = 2 ** j
        return to_peer(gathered.at[pl.ds(0, size)], gathered.at[pl.ds(size, size)],
                       ring_send.at[j], ring_recv.at[j], stages[j])

    def swap_c(m):
        return to_peer(shared_c.at[m, 0], shared_c.at[m, 1], pair_send.at[m], pair_recv.at[m],
                       {"t": 1 - at_t})

    def swap_r(m, s):
        here = pl.ds(pl.multiple_of(s * rows, 16), rows)
        return to_peer(shared_r.at[m, 0, here], shared_r.at[m, 1, here], pair_send_r.at[m, s],
                       pair_recv_r.at[m, s], {"t": 1 - at_t})

    def relative(r):
        o = flipped_if(at_o, 1, lax.rem(r // 2, 2))
        i = flipped_if(at_i, 4, lax.rem(r // 4, 2))
        i = flipped_if(i, 2, lax.rem(r // 8, 2))
        i = flipped_if(i, 1, lax.rem(r // 16, 2))
        return o, i, flipped_if(at_t, 1, lax.rem(r, 2))

    def opening(tok, cot, proj, mixed, gates):
        fill = pltpu.make_async_copy(pack_ref, gathered.at[0], load.at[0])
        take_cot = pltpu.make_async_copy(cot_ref, cot, load.at[1])
        take_tok = pltpu.make_async_copy(tok_ref, tok, load.at[2])
        fill.start()
        take_cot.start()
        take_tok.start()
        fill.wait()
        stage(0).start()
        take_cot.wait()
        shared_c[0, 0] = cot[0:images // 2].reshape(own_rows, width).astype(jnp.bfloat16)
        swap_c(0).start()
        stage(0).wait()
        stage(1).start()
        shared_c[1, 0] = cot[images // 2:].reshape(own_rows, width).astype(jnp.bfloat16)
        swap_c(1).start()
        stage(1).wait()
        stage(2).start()
        stage(2).wait()
        stage(3).start()
        weights.send(0)
        swap_c(0).wait()
        cot_plan.send(0)
        stage(3).wait()
        stage(4).start()
        swap_c(1).wait()
        cot_plan.send(1)
        stage(4).wait()

        def place(r, carry):
            o, i, t = relative(r)
            row = pl.multiple_of((o * 8 + i) * depth, depth)
            for c in range(kinds):
                mats_ref[t, c, pl.ds(row, depth)] = gathered[r, c * depth:(c + 1) * depth]
            loose[(o * 8 + i) * 2 + t] = gathered[r, kinds * depth:, 0:LANES].astype(jnp.float32)
            return carry

        lax.fori_loop(0, gathered.shape[0], place, 0)
        turned = loose[...].reshape(width, LANES).T
        norms_ref[...] = turned[96:104] + turned[104:112] + turned[112:120]
        low = turned[0:96].astype(jnp.bfloat16)
        parts_ref[...] = jnp.concatenate([low, jnp.zeros((32, width), jnp.bfloat16)], 0)
        router_ref[0:32] = turned[0:32] + turned[32:64] + turned[64:96]
        router_ref[32:] = jnp.zeros((96, width), jnp.float32)
        take_tok.wait()

        def attend(n, carry):
            m, s = n // steps, lax.rem(n, steps)
            _, routed = forward_rows(n * per_step, per_step, tok, bias_ref, mats_ref, norms_ref, parts_ref,
                                     tok, proj, mixed, gates)
            shared_r[m, 0, pl.ds(pl.multiple_of(s * rows, 16), rows)] = routed
            swap_r(m, s).start()
            return carry

        lax.fori_loop(0, micros * steps, attend, 0)
        outs = [(tok, middle_out), (proj, proj_out), (mixed, mixed_out), (gates, gates_out)]
        stores = [pltpu.make_async_copy(a, b, store.at[n]) for n, (a, b) in enumerate(outs)]
        for copy in stores:
            copy.start()
        for m in range(micros):
            for s in range(steps):
                swap_r(m, s).wait()
            row_plan.send(m)
        weights.send(1)
        for copy in stores:
            copy.wait()

    pl.run_scoped(
        opening,
        pltpu.VMEM(tok_ref.shape, jnp.float32),
        pltpu.VMEM(cot_ref.shape, jnp.float32),
        pltpu.VMEM((images, length, 3 * width), jnp.bfloat16),
        pltpu.VMEM((images, length, width), jnp.bfloat16),
        pltpu.VMEM((images, length, LANES), jnp.float32),
    )
    for m in range(micros):
        row_plan.finish(m)
        cot_plan.finish(m)
    back = Answer(staged_back, back_ref, back_send, back_recv, back_keep, 8)
    result = Answer(staged_c, result_ref, result_send, result_recv, result_keep, 8)
    count = slots_ref.shape[1]

    def experts(*scratch):
        def one(k, carry):
            weights.finish(k)
            expert = (at_i * 2 + at_t) * local + k
            expert_phase(k, expert, slots_ref, cots_ref, held, parts_ref, (back, result), scratch)
            gradients.send(k)
            return carry

        lax.fori_loop(0, local, one, 0)

    pl.run_scoped(experts, *expert_scratch(count, width, 512, 480))

    places = lax.broadcasted_iota(jnp.int32, (1, 8 * CAP), 1)
    block = sum((places >= q * CAP).astype(jnp.int32) for q in range(1, 8))
    places = places + block * (3 * CAP) + at_t * (2 * CAP)

    def taken(table, m, half, here, values):
        first, second = table[m, half, here, 0:1], table[m, half, here, 1:2]
        total = None
        for k in range(local):
            where = places + k * CAP
            hits = jnp.where((first == where) | (second == where), 1.0, 0.0).astype(jnp.bfloat16)
            part = mm(hits, values[k])
            total = part if total is None else total + part
        return total

    across = {"t": 1 - at_t}

    def away(m, s, which):
        here = pl.ds(pl.multiple_of(s * rows, 16), rows)
        buffer = (shared_r, away_g, shared_c)[which]
        return to_peer(buffer.at[m, 0, here], buffer.at[m, 1, here], away_send.at[which, m, s],
                       away_recv.at[which, m, s], across)

    def collect(own):
        def fetched(table, backs, results):
            take = pltpu.make_async_copy(table_ref, table, fetch.at[2])
            take.start()
            take.wait()
            for m in range(micros):
                for k in range(local):
                    back.finish(k, m)
                    pltpu.make_async_copy(back_ref.at[k, m], backs.at[k], fetch.at[k]).start()
                for k in range(local):
                    pltpu.make_async_copy(back_ref.at[k, m], backs.at[k], fetch.at[k]).wait()

                def leave(s, carry):
                    here = pl.ds(pl.multiple_of(s * rows, 16), rows)
                    total = taken(table, m, 1, here, backs).astype(jnp.bfloat16)
                    shared_r[m, 0, here] = total[:, :width]
                    away_g[m, 0, here] = total[:, width:]
                    away(m, s, 0).start()
                    away(m, s, 1).start()
                    return carry

                lax.fori_loop(0, steps, leave, 0)

                def stay(s, carry):
                    here = pl.ds(pl.multiple_of(s * rows, 16), rows)
                    own[m * steps + s] = taken(table, m, 0, here, backs)
                    return carry

                lax.fori_loop(0, steps, stay, 0)
            for m in range(micros):
                for k in range(local):
                    result.finish(k, m)
                    pltpu.make_async_copy(result_ref.at[k, m], results.at[k], fetch.at[k]).start()
                for k in range(local):
                    pltpu.make_async_copy(result_ref.at[k, m], results.at[k], fetch.at[k]).wait()

                def leave(s, carry):
                    here = pl.ds(pl.multiple_of(s * rows, 16), rows)
                    shared_c[m, 0, here] = taken(table, m, 1, here, results).astype(jnp.bfloat16)
                    away(m, s, 2).start()
                    return carry

                lax.fori_loop(0, steps, leave, 0)

        pl.run_scoped(
            fetched, pltpu.VMEM(table_ref.shape, jnp.int32), pltpu.VMEM((local, 8 * CAP, width + LANES), jnp.bfloat16),
            pltpu.VMEM((local, 8 * CAP, width), jnp.bfloat16))

        def backward(tok, middle, cot, proj, mixed, gates, dproj, dmats, dnorms, drouter):
            dmats[...] = jnp.zeros_like(dmats)
            dnorms[...] = jnp.zeros_like(dnorms)
            drouter[...] = jnp.zeros_like(drouter)
            pairs = [(tok_ref, tok), (middle_out, middle), (cot_ref, cot), (proj_out, proj),
                     (mixed_out, mixed), (gates_out, gates)]

            def micro(m, carry):
                ours = pl.ds(m * (images // micros), images // micros)
                takes = [pltpu.make_async_copy(a.at[ours], b, fetch.at[n]) for n, (a, b) in enumerate(pairs)]
                for copy in takes:
                    copy.start()
                for copy in takes:
                    copy.wait()

                def attend(s, inside):
                    away(m, s, 0).wait()
                    away(m, s, 1).wait()
                    here = pl.ds(pl.multiple_of(s * rows, 16), rows)
                    grad = own[m * steps + s] + jnp.concatenate([
                        shared_r[m, 1, here].astype(jnp.float32), away_g[m, 1, here].astype(jnp.float32)], 1)
                    backward_rows(s * per_step, per_step, grad, tok, middle, cot, gates, proj, mixed,
                                  bias_ref.at[ours], mats_ref, norms_ref, router_ref, cot, dnorms, drouter,
                                  dproj, dmats)
                    return inside

                lax.fori_loop(0, steps, attend, 0)
                keep = pltpu.make_async_copy(cot, input_out.at[ours], store.at[0])
                keep.start()
                keep.wait()
                return carry

            lax.fori_loop(0, micros, micro, 0)
            tail = jnp.concatenate(
                [jnp.zeros((96, width), jnp.float32), dnorms[...], jnp.zeros((24, width), jnp.float32)], 0)
            drouter[...] += tail.T

            def spread(r, carry):
                o, i, t = relative(r)
                row = pl.multiple_of((o * 8 + i) * depth, depth)
                for c in range(kinds):
                    gathered[r, c * depth:(c + 1) * depth] = dmats[t, c, pl.ds(row, depth)].astype(jnp.bfloat16)
                row = pl.multiple_of(((o * 8 + i) * 2 + t) * 16, 16)
                gathered[r, kinds * depth:, 0:LANES] = drouter[pl.ds(row, 16)].astype(jnp.bfloat16)
                gathered[r, kinds * depth:, LANES:] = jnp.zeros((16, columns - LANES), jnp.bfloat16)
                return carry

            lax.fori_loop(0, gathered.shape[0], spread, 0)

        some = images // micros
        pl.run_scoped(
            backward,
            pltpu.VMEM((some, length, width), jnp.float32),
            pltpu.VMEM((some, length, width), jnp.float32),
            pltpu.VMEM((some, length, width), jnp.float32),
            pltpu.VMEM((some, length, 3 * width), jnp.bfloat16),
            pltpu.VMEM((some, length, width), jnp.bfloat16),
            pltpu.VMEM((some, length, LANES), jnp.float32),
            pltpu.VMEM((rows, 3 * width), jnp.float32),
            pltpu.VMEM(mats_ref.shape, jnp.float32),
            pltpu.VMEM((8, width), jnp.float32),
            pltpu.VMEM((width, LANES), jnp.float32),
        )

    pl.run_scoped(collect, pltpu.VMEM((micros * steps, rows, width + LANES), jnp.float32))

    def fold(j):
        size = 2 ** j
        return to_peer(gathered.at[pl.ds(size, size)], partial.at[pl.ds(size, size)],
                       fold_send.at[j], fold_recv.at[j], stages[j])

    def folded(j):
        fold(j).wait()
        size = 2 ** j

        def add(r, carry):
            gathered[r] = (gathered[r].astype(jnp.float32) + partial[size + r].astype(jnp.float32)).astype(
                jnp.bfloat16)
            return carry

        lax.fori_loop(0, size, add, 0)

    def outputs(table, middle, results):
        fold(4).start()
        index_take = pltpu.make_async_copy(table_ref, table, fetch.at[3])
        index_take.start()
        take = pltpu.make_async_copy(middle_out, middle, fetch.at[2])
        take.start()
        for m in range(micros):
            for k in range(local):
                pltpu.make_async_copy(result_ref.at[k, m], results.at[k], fetch.at[k]).start()
            for k in range(local):
                pltpu.make_async_copy(result_ref.at[k, m], results.at[k], fetch.at[k]).wait()
            if m == 0:
                take.wait()
                index_take.wait()

            def stay(s, carry):
                n = m * steps + s
                here = pl.ds(pl.multiple_of(s * rows, 16), rows)
                away(m, s, 2).wait()
                total = taken(table, m, 0, here, results) + shared_c[m, 1, here].astype(jnp.float32)
                images_here = pl.ds(n * per_step, per_step)
                middle[images_here] = middle[images_here] + total.reshape(per_step, length, width)
                return carry

            lax.fori_loop(0, steps, stay, 0)
            folded(4 - m)
            fold(3 - m).start()
        keep = pltpu.make_async_copy(middle, block_out, store.at[0])
        keep.start()
        for j in (2, 1):
            folded(j)
            fold(j - 1).start()
        fold(0).wait()
        small_ref[...] = gathered[0].astype(jnp.float32) + partial[1].astype(jnp.float32)
        keep.wait()

    pl.run_scoped(
        outputs, pltpu.VMEM(table_ref.shape, jnp.int32), pltpu.VMEM(tok_ref.shape, jnp.float32),
        pltpu.VMEM((local, 8 * CAP, width), jnp.bfloat16))

    def close(k, carry):
        gradients.finish(k)
        return carry

    lax.fori_loop(0, local, close, 0)


def opening(pack, cot, index, table, tok, bias, first_in, second_in, local, per_step):
    micros, own_rows = index.shape[0], index.shape[3]
    images, length, width = tok.shape
    columns = pack.shape[1]
    experts, depth, extent = first_in.shape
    steps = own_rows // (per_step * length)
    slots = micros * 8 * CAP
    anywhere = pl.BlockSpec(memory_space=pl.ANY)
    vector = pl.BlockSpec(memory_space=pltpu.VMEM)
    dma = pltpu.SemaphoreType.DMA
    low, wide = jnp.bfloat16, jnp.float32
    weights = (local, 2, 8, 2, 2, depth, extent)
    shape = jax.ShapeDtypeStruct
    return pl.pallas_call(
        functools.partial(opening_kernel, local, per_step),
        in_specs=[anywhere, anywhere, vector, anywhere, anywhere, vector, anywhere, anywhere],
        out_specs=[vector] + [anywhere] * 11,
        out_shape=[
            shape(pack.shape, wide), shape(tok.shape, wide), shape(tok.shape, wide),
            shape((2, experts, 2, depth, extent), low),
            shape((images, length, width), wide), shape((images, length, 3 * width), low),
            shape((images, length, width), low), shape((images, length, LANES), wide),
            shape((local, slots, width), low), shape((local, slots, width), low),
            shape((local, micros, 8 * CAP, width + LANES), low), shape((local, micros, 8 * CAP, width), low),
        ],
        scratch_shapes=[
            pltpu.VMEM((32,) + pack.shape, low),
            pltpu.VMEM((32,) + pack.shape, low),
            pltpu.VMEM((32, width // 32, LANES), wide),
            pltpu.VMEM((2, 4, width, columns), low), pltpu.VMEM((8, width), wide),
            pltpu.VMEM((LANES, width), low), pltpu.VMEM((LANES, width), wide),
            pltpu.VMEM((micros, 2, own_rows, width), low),
            pltpu.VMEM((micros, 2, own_rows, width), low),
            pltpu.VMEM((micros, 2, own_rows, LANES), low),
            pltpu.VMEM((micros, 8, local, CAP, width), low),
            pltpu.VMEM((micros, 8, local, CAP, width), low),
            pltpu.VMEM(weights, low),
            pltpu.VMEM((micros, 8, local, CAP, width + LANES), low),
            dma((3,)), dma((5,)), dma((5,)), dma((micros,)), dma((micros,)),
            dma((micros, steps)), dma((micros, steps)),
            dma((micros, 8, local)), dma((micros, 8, local)), dma((micros, local)),
            dma((micros, 8, local)), dma((micros, 8, local)), dma((micros, local)),
            dma((local, 32, 2)), dma((local, 32, 2)), dma((local, 2)),
            dma((local, 32, 2)), dma((local, 32, 2)), dma((local, 2)),
            dma((local, micros, 8)), dma((local, micros, 8)), dma((local, micros)),
            dma((local, micros, 8)), dma((local, micros, 8)), dma((local, micros)), dma((4,)),
            dma((3, micros, steps)), dma((3, micros, steps)), dma((5,)), dma((5,)), dma((6,)),
        ],
        compiler_params=pltpu.CompilerParams(vmem_limit_bytes=67043328, has_side_effects=True),
        cost_estimate=pl.CostEstimate(flops=1000, bytes_accessed=1000, transcendentals=0),
        name="opening",
    )(pack, cot, index, table, tok, bias, first_in, second_in)


def per_device(planes, inner, parts, tokens, key_mask, expert_ids, slot_ids, norm1_gain, norm1_bias,
               qkv_weight, out_weight, norm2_gain, norm2_bias, router_weight, expert_in, expert_out,
               cotangent):
    micros, own_rows, width = tokens.shape
    length = key_mask.shape[2]
    group_rows = own_rows * parts
    images = own_rows // length
    total = micros * images
    experts = expert_in.shape[0]
    homes = inner * parts
    local = experts // homes
    depth, extent = expert_in.shape[1:]
    small = norm1_gain.shape[0]
    every = ("o", "i", "t")
    plane_at, inner_at, part_at = (lax.axis_index(name) for name in every)
    low = jnp.bfloat16

    loose = jnp.concatenate([
        jnp.stack([norm1_gain, norm1_bias, norm2_gain, norm2_bias], 1), router_weight], 1)
    loose_count = 3 * loose.size
    columns = qkv_weight.shape[2]
    loose_rows = -(-loose_count // (16 * columns)) * 16
    loose_low = jnp.concatenate([p.reshape(-1) for p in three_parts(loose)])
    loose_low = jnp.pad(loose_low, (0, loose_rows * columns - loose_count)).reshape(loose_rows, columns)
    packed = jnp.concatenate([
        qkv_weight.transpose(1, 0, 2).reshape(3 * depth, columns), out_weight.T, loose_low], 0)
    gathered = lax.all_gather(packed, ("o", "i"), axis=0)
    gathered = lax.all_gather(gathered, "t", axis=0)
    mats = gathered[:, :, :4 * depth].reshape(parts, planes * inner, 4, depth, columns)
    mats = mats.transpose(2, 1, 3, 0, 4).reshape(1, 4, width, width)
    loose_all = gathered[:, :, 4 * depth:].reshape(parts, planes * inner, loose_rows * columns)
    loose_all = loose_all[:, :, :loose_count].astype(jnp.float32)
    loose_all = loose_all.reshape(parts, planes * inner, 3, small, 4 + experts)
    loose_all = (loose_all[:, :, 0] + loose_all[:, :, 1]) + loose_all[:, :, 2]
    loose_all = loose_all.transpose(1, 0, 2, 3).reshape(width, 4 + experts)
    norms = loose_all[:, :4].T
    router = jnp.pad(loose_all[:, 4:], ((0, 0), (0, LANES - experts)))
    router_parts = jnp.concatenate(three_parts(router[:, :experts]), 1).T
    router_parts = jnp.pad(router_parts, ((0, LANES - 3 * experts), (0, 0)))

    weights = []
    first_in = expert_in.reshape(homes, local, depth, extent)
    second_in = expert_out.transpose(0, 2, 1).reshape(homes, local, depth, extent)
    for k in range(local):
        both = jnp.stack([first_in[:, k], second_in[:, k]], 1)
        mine = lax.all_to_all(both, ("i", "t"), 0, 0, tiled=True)
        if planes == 2:
            other = lax.ppermute(mine, "o", [(0, 1), (1, 0)])
            full = jnp.where(plane_at == 0, jnp.stack([mine, other]), jnp.stack([other, mine]))
        else:
            full = lax.all_gather(mine, "o", axis=0)
        weights.append(full.reshape(planes, inner, parts, 2, depth, extent))

    own_first = part_at * own_rows
    slot_index = jnp.where(slot_ids >= 0, expert_ids * CAP + slot_ids, -1)
    if parts == 2:
        slot_index = jnp.concatenate([
            lax.dynamic_slice_in_dim(slot_index, own_first, own_rows, 1),
            lax.dynamic_slice_in_dim(slot_index, own_rows - own_first, own_rows, 1)], 1)
    homes_i = lax.broadcasted_iota(jnp.int32, (inner, local, CAP), 0)
    locals_i = lax.broadcasted_iota(jnp.int32, (inner, local, CAP), 1)
    cap_i = lax.broadcasted_iota(jnp.int32, (inner, local, CAP), 2)
    places = ((homes_i * parts + part_at) * local + locals_i) * CAP + cap_i

    def table(m, positions, rows=slice(None)):
        index = slot_index[m, rows]
        flat = positions.reshape(1, -1)
        return ((index[:, 0:1] == flat) | (index[:, 1:2] == flat)).astype(low)

    def share(rows):
        if parts == 2:
            return jnp.concatenate([rows, lax.ppermute(rows, "t", [(0, 1), (1, 0)])], 1)
        return lax.all_gather(rows, "t", axis=1, tiled=True)

    def dispatch(shared):
        sent = []
        for m in range(micros):
            slots = mm(table(m, places), shared[m], TN).astype(low)
            slots = lax.all_to_all(slots.reshape(inner, local * CAP, width), "i", 0, 0, tiled=True)
            sent.append(slots.reshape(inner, local, CAP, width))
        return [
            jnp.concatenate([s[:, k].reshape(inner * CAP, width) for s in sent], 0) for k in range(local)]

    cot_slots = dispatch(share(cotangent.astype(low)))

    flags = lax.dynamic_slice_in_dim(key_mask, part_at * images, images, 1).reshape(total, 1, length)
    bias = jnp.where(flags > 0, 0.0, -1e30).astype(jnp.float32)
    tok = tokens.reshape(total, length, width)
    per_step = 2 if total % 2 == 0 else 1
    middle, routed, proj, mixed, gates = attention_forward(tok, bias, mats, norms, router_parts, per_step)

    row_slots = dispatch(share(routed.reshape(micros, own_rows, width)))

    first_out, second_out, results, backs = [], [], [], []
    for k in range(local):
        expert = ((inner_at * parts + part_at) * local + k).astype(jnp.int32).reshape(1)
        result, back, dweights = run_expert(expert, row_slots[k], cot_slots[k], weights[k], router_parts)
        results.append(result.reshape(micros, inner, CAP, width))
        backs.append(back.reshape(micros, inner, CAP, width + LANES))
        dweights = dweights.reshape(planes, homes, 2, depth, extent)
        if planes == 2:
            theirs = lax.dynamic_index_in_dim(dweights, 1 - plane_at, 0, keepdims=False)
            ours = lax.dynamic_index_in_dim(dweights, plane_at, 0, keepdims=False)
            summed = ours.astype(jnp.float32) + lax.ppermute(
                theirs, "o", [(0, 1), (1, 0)]).astype(jnp.float32)
            summed = summed.astype(low)
        else:
            summed = lax.psum_scatter(dweights, "o", scatter_dimension=0, tiled=True)[0]
        final = lax.all_to_all(summed, ("i", "t"), 0, 0, tiled=True)
        first_out.append(final[:, 0])
        second_out.append(final[:, 1])
    first_grad = jnp.stack(first_out, 1).reshape(experts, depth, extent).astype(jnp.float32)
    second_grad = jnp.stack(second_out, 1).reshape(experts, depth, extent).astype(jnp.float32)
    second_grad = second_grad.transpose(0, 2, 1)

    def collect(values):
        size = values[0].shape[-1]
        answers = []
        for m in range(micros):
            back = jnp.stack([v[m] for v in values], 1).reshape(inner, local * CAP, size)
            back = lax.all_to_all(back, "i", 0, 0, tiled=True).reshape(inner * local * CAP, size)
            if parts == 2:
                away = mm(table(m, places, slice(own_rows, None)), back).astype(low)
                here = mm(table(m, places, slice(0, own_rows)), back)
                answers.append(here + lax.ppermute(away, "t", [(0, 1), (1, 0)]).astype(jnp.float32))
            else:
                whole = mm(table(m, places), back).astype(low)
                answers.append(lax.psum_scatter(
                    whole, "t", scatter_dimension=0, tiled=True).astype(jnp.float32))
        return jnp.stack(answers)

    grad = collect(backs)
    combined = collect(results)
    block_out = middle.reshape(micros, own_rows, width) + combined

    input_grad, dmats, dnorms, drouter = attention_backward(
        tok, middle, cotangent.reshape(total, length, width), grad.reshape(total, length, width + LANES),
        gates, proj, mixed, bias, mats, norms, router.T, per_step)
    input_grad = input_grad.reshape(micros, own_rows, width)

    dmats = dmats.reshape(4, planes, inner, depth, parts, columns).transpose(2, 4, 1, 0, 3, 5)
    dmats = dmats.reshape(homes, planes, 4 * depth, columns)
    dloose = jnp.concatenate([dnorms.T, drouter[:, :experts]], 1)
    dloose = dloose.reshape(planes, inner, parts, small * (4 + experts)).transpose(1, 2, 0, 3)
    dloose = jnp.concatenate(three_parts(dloose), -1)
    dloose = jnp.pad(dloose, ((0, 0),) * 3 + ((0, loose_rows * columns - loose_count),))
    dloose = dloose.reshape(homes, planes, loose_rows, columns)
    payload = jnp.concatenate([dmats, dloose], 2)
    payload = lax.all_to_all(payload, ("i", "t"), 0, 0, tiled=True)
    payload = jnp.sum(payload.astype(jnp.float32), 0)
    if planes == 2:
        theirs = lax.dynamic_index_in_dim(payload, 1 - plane_at, 0, keepdims=False)
        ours = lax.dynamic_index_in_dim(payload, plane_at, 0, keepdims=False)
        reduced = ours + lax.ppermute(theirs, "o", [(0, 1), (1, 0)])
    else:
        reduced = lax.psum_scatter(payload, "o", scatter_dimension=0, tiled=True)[0]
    matrices = reduced[:4 * depth].reshape(4, depth, columns)
    qkv_grad = matrices[:3].transpose(1, 0, 2)
    out_grad = matrices[3].T
    tail = reduced[4 * depth:].reshape(-1)[:loose_count].reshape(3, small, 4 + experts)
    tail = (tail[0] + tail[1]) + tail[2]
    return (
        block_out, input_grad, tail[:, 0], tail[:, 1], qkv_grad, out_grad, tail[:, 2], tail[:, 3],
        tail[:, 4:], first_grad, second_grad,
    )


def per_device_halves(tokens, key_mask, expert_ids, slot_ids, norm1_gain, norm1_bias,
                      qkv_weight, out_weight, norm2_gain, norm2_bias, router_weight, expert_in, expert_out,
                      cotangent):
    micros, own_rows, width = tokens.shape
    length = key_mask.shape[2]
    images = own_rows // length
    total = micros * images
    planes, inner, parts = 2, 8, 2
    experts = expert_in.shape[0]
    homes = inner * parts
    local = experts // homes
    depth, extent = expert_in.shape[1:]
    columns = qkv_weight.shape[2]
    plane_at, inner_at, part_at = (lax.axis_index(name) for name in ("o", "i", "t"))
    low = jnp.bfloat16
    across = [(0, 1), (1, 0)]

    norms_in = jnp.stack([norm1_gain, norm1_bias, norm2_gain, norm2_bias], 1)
    loose = [p for p in three_parts(router_weight)]
    loose += [jnp.pad(p, ((0, 0), (0, 4))) for p in three_parts(norms_in)]
    loose = jnp.concatenate(loose, 1)
    loose = jnp.pad(loose, ((0, 0), (0, columns - loose.shape[1])))
    packed = jnp.concatenate([
        qkv_weight.transpose(1, 0, 2).reshape(3 * depth, columns), out_weight.T, loose], 0)
    slot_index = jnp.where(slot_ids >= 0, expert_ids * CAP + slot_ids, -1).transpose(0, 2, 1)
    own_first = part_at * own_rows
    index = jnp.stack([
        lax.dynamic_slice_in_dim(slot_index, own_first, own_rows, 2),
        lax.dynamic_slice_in_dim(slot_index, own_rows - own_first, own_rows, 2)], 2)

    flags = lax.dynamic_slice_in_dim(key_mask, part_at * images, images, 1).reshape(total, 1, length)
    bias = jnp.where(flags > 0, 0.0, -1e30).astype(jnp.float32)
    tok = tokens.reshape(total, length, width)
    table = jnp.pad(index.transpose(0, 2, 3, 1), ((0, 0), (0, 0), (0, 0), (0, LANES - 2)))
    reduced, block_out, input_grad, dweights = opening(
        packed, cotangent.reshape(tok.shape), index, table, tok, bias, expert_in, expert_out.transpose(0, 2, 1), local, 2)[:4]
    dweights = dweights[0].astype(jnp.float32) + dweights[1].astype(jnp.float32)
    first_grad = dweights[:, 0]
    second_grad = dweights[:, 1].transpose(0, 2, 1)
    matrices = reduced[:4 * depth].reshape(4, depth, columns)
    qkv_grad = matrices[:3].transpose(1, 0, 2)
    out_grad = matrices[3].T
    tail = reduced[4 * depth:]
    shape = (micros, own_rows, width)
    return (
        block_out.reshape(shape), input_grad.reshape(shape), tail[:, 96], tail[:, 97], qkv_grad, out_grad,
        tail[:, 98], tail[:, 99], tail[:, :experts], first_grad, second_grad,
    )


def solution(mesh):
    dp, parts = mesh.shape["dp"], mesh.shape["tensor"]
    inner = min(8, 32 // parts, dp)
    planes = dp // inner
    fine = Mesh(mesh.devices.reshape(planes, inner, parts), ("o", "i", "t"))
    dps = ("o", "i")
    every = ("o", "i", "t")
    rows = P(None, every, None)
    step = functools.partial(per_device, planes, inner, parts)
    if (planes, inner, parts) == (2, 8, 2):
        step = per_device_halves
    return jax.shard_map(
        step,
        mesh=fine,
        in_specs=(
            rows, P(None, dps, None), P(None, dps, None), P(None, dps, None), P(every), P(every),
            P(dps, None, "t"), P("t", dps), P(every), P(every), P(every, None),
            P(None, dps, "t"), P(None, "t", dps), rows,
        ),
        out_specs=(
            rows, rows, P(every), P(every), P(dps, None, "t"), P("t", dps), P(every), P(every),
            P(every, None), P(None, dps, "t"), P(None, "t", dps),
        ),
        check_vma=False,
    )
```

profile of v0, /device:TPU:26, one launch (start us, length us, event | category | flops | bytes accessed | tf_op | source)
XLA Modules:
  0.0 611.7 jit_solution(11030386800711425798)
XLA Ops:
  0.6 0.7 fusion.5
  1.4 0.7 pad_maximum_fusion
  2.1 0.1 copy.60
  2.2 0.1 copy.62
  2.3 0.7 fusion.2
  3.0 0.6 select_n.24.bias_ref
  3.6 0.8 subtract_convert_fusion.1
  4.4 0.1 concatenate.6
  4.5 0.8 broadcast_compare_fusion
  5.3 0.8 broadcast_multiply_fusion
  6.0 1.5 fusion.1.pack_ref
  7.5 1.3 copy.65
  8.8 0.5 copy.63
  9.3 1.3 copy.64
  10.6 1.2 add_select_fusion
  11.8 0.1 dynamic-slice_bitcast_fusion.1
  11.9 0.2 fusion.6
  12.2 1.3 pad.22.table_ref
  13.4 1.2 copy.67.index_ref
  14.6 576.2 %opening.1 = (f32[144,256]{1,0:T(8,128)}, f32[8,200,512]{2,1,0:T(8,128)}, f32[8,200,512]{2,1,0:T(8,128)}, bf16[2,32,2,32,1024]{4,3,2,1,0:T(8,128)(2,1)}, f32[8,2...) custom-call(bf16[144,256]{1,0:T(8,128)(2,1)} %fusion.1.pack_ref, ...), custom_call_target="tpu_custom_call" | custom-call | flops 1000 | bytes 1000 | tf_op jit(solution)/shard_map/opening/pallas_call | solution.py:1043
  590.8 1.6 slice_reduce_fusion
  592.4 1.3 slice.53
  593.7 1.4 slice_bitcast_fusion.2
  595.1 1.5 slice.48
  596.6 5.6 add_bitcast_fusion
  602.2 0.0 copy-start.1
  602.2 4.3 slice_bitcast_fusion
  606.5 0.0 copy-done.1
  606.5 0.0 copy-start
  606.5 1.7 copy.70
  608.2 1.4 copy-done
  609.6 1.7 copy.71
  (4 shorter events, 0.0 us)
Async XLA Ops:
  602.2 4.3 copy-start.1
  606.5 3.1 copy-start
where the time goes:
time: 622 us; the launch traced here: 612 us
  Pallas kernels  576 us (93%)
  local copies, waits for them, and re-layouts  21.4 us (3%)
  other arithmetic  12.9 us (2%)
    pallas_call x1, Pallas kernels, opening(): pl.pallas_call(functools.partial(opening_kernel, local, per_step), in_spe...  576 us

commit v1 on v0

--- a/solution.py
+++ b/solution.py
@@ -453,11 +453,13 @@
         for k in range(self.local):
             self.staged[m, d, k] = total[k * CAP:(k + 1) * CAP].astype(jnp.bfloat16)
 
-    def send(self, m):
+    def send(self, m, beside=None):
         def step(d, carry):
             self.fill(m, d)
             for k in range(self.local):
                 self.copy(m, d, k).start()
+            if beside is not None:
+                beside(d)
             return carry
 
         lax.fori_loop(1, self.inner, step, 0)
@@ -497,9 +499,11 @@
     def kept(self, k, m):
         return pltpu.make_async_copy(self.staged.at[m, self.at_i, k], self.target(k, m), self.keep.at[k, m])
 
-    def send(self, k, m):
+    def send(self, k, m, beside=None):
         def step(d, carry):
             self.copy(k, m, d).start()
+            if beside is not None:
+                beside(d)
             return carry
 
         lax.fori_loop(1, self.inner, step, 0)
@@ -541,13 +545,18 @@
         return pltpu.make_async_copy(
             self.sources[part].at[expert], self.place(k, part), self.keep.at[k, part])
 
-    def send(self, k):
+    def give(self, k, n):
+        for part in range(2):
+            self.copy(k, n, part).start()
+
+    def give_all(self, k, first, last):
         def step(n, carry):
-            for part in range(2):
-                self.copy(k, 32 - n, part).start()
+            self.give(k, n)
             return carry
 
-        lax.fori_loop(1, 32, step, 0)
+        lax.fori_loop(first, last, step, 0)
+
+    def keep_own(self, k):
         for part in range(2):
             self.kept(k, part).start()
 
@@ -582,7 +591,9 @@
         return pltpu.make_async_copy(
             self.source.at[k, o, i, t, part], self.place(k, part), self.keep.at[k, part])
 
-    send = Weights.send
+    give = Weights.give
+    give_all = Weights.give_all
+    keep_own = Weights.keep_own
     finish = Weights.finish
 
 
@@ -598,7 +609,7 @@
     ]
 
 
-def expert_phase(k, expert, slots_hbm, cots_hbm, held, parts_ref, answers, scratch):
+def expert_phase(k, expert, slots_hbm, cots_hbm, held, parts_ref, answers, gradients, scratch):
     slots, cots, rows_t, grads_t, grads, gate_scr, result_acc, back_acc, sums, tiles, load = scratch
     count, width = slots.shape
     chunk = rows_t.shape[2]
@@ -679,10 +690,18 @@
         return carry
 
     lax.fori_loop(0, micros * groups // per_chunk, finish, 0)
+
+    def one_more(d):
+        @pl.when(k == 0)
+        def _():
+            gradients.give(0, 15 + d)
+
     for m in range(micros):
-        back.send(k, m)
-    for m in range(micros):
-        result.send(k, m)
+        back.send(k, m, one_more if m == 0 else None)
+
+    @pl.when(k == 0)
+    def _():
+        gradients.give_all(0, 23, 26)
 
 
 def opening_kernel(
@@ -754,13 +773,15 @@
         stage(2).start()
         stage(2).wait()
         stage(3).start()
-        weights.send(0)
+        weights.give_all(0, 30, 32)
         swap_c(0).wait()
-        cot_plan.send(0)
+        cot_plan.send(0, lambda d: weights.give(0, d + 15))
         stage(3).wait()
         stage(4).start()
         swap_c(1).wait()
-        cot_plan.send(1)
+        cot_plan.send(1, lambda d: weights.give(0, d + 22))
+        weights.give_all(0, 1, 16)
+        weights.keep_own(0)
         stage(4).wait()
 
         def place(r, carry):
@@ -796,8 +817,10 @@
         for m in range(micros):
             for s in range(steps):
                 swap_r(m, s).wait()
-            row_plan.send(m)
-        weights.send(1)
+            row_plan.send(m, (lambda d: weights.give(1, d + 15)) if m == 0 else None)
+        weights.give_all(1, 23, 32)
+        weights.give_all(1, 1, 16)
+        weights.keep_own(1)
         for copy in stores:
             copy.wait()
 
@@ -820,13 +843,26 @@
         def one(k, carry):
             weights.finish(k)
             expert = (at_i * 2 + at_t) * local + k
-            expert_phase(k, expert, slots_ref, cots_ref, held, parts_ref, (back, result), scratch)
-            gradients.send(k)
+            expert_phase(k, expert, slots_ref, cots_ref, held, parts_ref, (back, result), gradients, scratch)
             return carry
 
         lax.fori_loop(0, local, one, 0)
 
     pl.run_scoped(experts, *expert_scratch(count, width, 512, 480))
+
+    gradients.give_all(0, 26, 32)
+    result.send(0, 0, lambda d: gradients.give(1, 15 + d))
+    result.send(0, 1, lambda d: gradients.give(1, 22 + d))
+    gradients.give_all(1, 30, 32)
+    for m in range(micros):
+        result.send(1, m)
+
+    def rest(k, carry):
+        gradients.give_all(k, 1, 16)
+        gradients.keep_own(k)
+        return carry
+
+    lax.fori_loop(0, local, rest, 0)
 
     places = lax.broadcasted_iota(jnp.int32, (1, 8 * CAP), 1)
     block = sum((places >= q * CAP).astype(jnp.int32) for q in range(1, 8))
@@ -851,7 +887,7 @@
                        away_recv.at[which, m, s], across)
 
     def collect(own):
-        def fetched(table, backs, results):
+        def fetched(table, backs):
             take = pltpu.make_async_copy(table_ref, table, fetch.at[2])
             take.start()
             take.wait()
@@ -879,24 +915,9 @@
                     return carry
 
                 lax.fori_loop(0, steps, stay, 0)
-            for m in range(micros):
-                for k in range(local):
-                    result.finish(k, m)
-                    pltpu.make_async_copy(result_ref.at[k, m], results.at[k], fetch.at[k]).start()
-                for k in range(local):
-                    pltpu.make_async_copy(result_ref.at[k, m], results.at[k], fetch.at[k]).wait()
-
-                def leave(s, carry):
-                    here = pl.ds(pl.multiple_of(s * rows, 16), rows)
-                    shared_c[m, 0, here] = taken(table, m, 1, here, results).astype(jnp.bfloat16)
-                    away(m, s, 2).start()
-                    return carry
-
-                lax.fori_loop(0, steps, leave, 0)
 
         pl.run_scoped(
-            fetched, pltpu.VMEM(table_ref.shape, jnp.int32), pltpu.VMEM((local, 8 * CAP, width + LANES), jnp.bfloat16),
-            pltpu.VMEM((local, 8 * CAP, width), jnp.bfloat16))
+            fetched, pltpu.VMEM(table_ref.shape, jnp.int32), pltpu.VMEM((local, 8 * CAP, width + LANES), jnp.bfloat16))
 
         def backward(tok, middle, cot, proj, mixed, gates, dproj, dmats, dnorms, drouter):
             dmats[...] = jnp.zeros_like(dmats)
@@ -986,27 +1007,41 @@
         index_take.start()
         take = pltpu.make_async_copy(middle_out, middle, fetch.at[2])
         take.start()
+        def load(m, k):
+            return pltpu.make_async_copy(result_ref.at[k, m], results.at[m, k], fetch.at[4 + k])
+
+        index_take.wait()
         for m in range(micros):
             for k in range(local):
-                pltpu.make_async_copy(result_ref.at[k, m], results.at[k], fetch.at[k]).start()
+                result.finish(k, m)
+                load(m, k).start()
             for k in range(local):
-                pltpu.make_async_copy(result_ref.at[k, m], results.at[k], fetch.at[k]).wait()
-            if m == 0:
-                take.wait()
-                index_take.wait()
-
+                load(m, k).wait()
+
+            def leave(s, carry):
+                here = pl.ds(pl.multiple_of(s * rows, 16), rows)
+                shared_c[m, 0, here] = taken(table, m, 1, here, results.at[m]).astype(jnp.bfloat16)
+                away(m, s, 2).start()
+                return carry
+
+            lax.fori_loop(0, steps, leave, 0)
+        folded(4)
+        fold(3).start()
+        take.wait()
+        for m in range(micros):
             def stay(s, carry):
                 n = m * steps + s
                 here = pl.ds(pl.multiple_of(s * rows, 16), rows)
                 away(m, s, 2).wait()
-                total = taken(table, m, 0, here, results) + shared_c[m, 1, here].astype(jnp.float32)
+                total = taken(table, m, 0, here, results.at[m]) + shared_c[m, 1, here].astype(jnp.float32)
                 images_here = pl.ds(n * per_step, per_step)
                 middle[images_here] = middle[images_here] + total.reshape(per_step, length, width)
                 return carry
 
             lax.fori_loop(0, steps, stay, 0)
-            folded(4 - m)
-            fold(3 - m).start()
+            if m == 0:
+                folded(3)
+                fold(2).start()
         keep = pltpu.make_async_copy(middle, block_out, store.at[0])
         keep.start()
         for j in (2, 1):
@@ -1018,7 +1053,7 @@
 
     pl.run_scoped(
         outputs, pltpu.VMEM(table_ref.shape, jnp.int32), pltpu.VMEM(tok_ref.shape, jnp.float32),
-        pltpu.VMEM((local, 8 * CAP, width), jnp.bfloat16))
+        pltpu.VMEM((micros, local, 8 * CAP, width), jnp.bfloat16))
 
     def close(k, carry):
         gradients.finish(k)

time: 622 us -> 575 us (0.924)
  the two profiles are of different devices: /device:TPU:26 before, /device:TPU:4 now
where the time goes in v1:
time: 575 us; the launch traced here: 564 us
  Pallas kernels  529 us (92%)
  local copies, waits for them, and re-layouts  21.4 us (4%)
  other arithmetic  12.9 us (2%)
    pallas_call x1, Pallas kernels, opening(): pl.pallas_call(functools.partial(opening_kernel, local, per_step), in_spe...  529 us

profile of v1, /device:TPU:4, one launch (start us, length us, event | category | flops | bytes accessed | tf_op | source)
XLA Modules:
  0.0 563.9 jit_solution(12064382752323502901)
XLA Ops:
  0.6 0.7 fusion.5
  1.4 0.7 pad_maximum_fusion
  2.1 0.1 copy.60
  2.2 0.1 copy.62
  2.3 0.7 fusion.2
  3.0 0.6 select_n.24.bias_ref
  3.6 0.8 subtract_convert_fusion.1
  4.4 0.1 concatenate.6
  4.5 0.8 broadcast_compare_fusion
  5.3 0.8 broadcast_multiply_fusion
  6.0 1.5 fusion.1.pack_ref
  7.5 1.3 copy.65
  8.8 0.5 copy.63
  9.3 1.3 copy.64
  10.6 1.2 add_select_fusion
  11.8 0.1 dynamic-slice_bitcast_fusion.1
  11.9 0.2 fusion.6
  12.2 1.3 pad.22.table_ref
  13.4 1.2 copy.67.index_ref
  14.6 528.7 %opening.1 = (f32[144,256]{1,0:T(8,128)}, f32[8,200,512]{2,1,0:T(8,128)}, f32[8,200,512]{2,1,0:T(8,128)}, bf16[2,32,2,32,1024]{4,3,2,1,0:T(8,128)(2,1)}, f32[8,2...) custom-call(bf16[144,256]{1,0:T(8,128)(2,1)} %fusion.1.pack_ref, ...), custom_call_target="tpu_custom_call" | custom-call | flops 1000 | bytes 1000 | tf_op jit(solution)/shard_map/opening/pallas_call | solution.py:1078
  543.3 1.6 slice_reduce_fusion
  544.9 1.3 slice.53
  546.2 1.4 slice_bitcast_fusion.2
  547.5 1.5 slice.48
  549.1 5.6 add_bitcast_fusion
  554.7 0.0 copy-start.1
  554.7 4.3 slice_bitcast_fusion
  558.9 0.0 copy-done.1
  558.9 0.0 copy-start
  558.9 1.7 copy.70
  560.6 1.4 copy-done
  562.1 1.7 copy.71
  (4 shorter events, 0.0 us)
Async XLA Ops:
  554.7 4.3 copy-start.1
  558.9 3.1 copy-start
